TPU v7x, 32 devices: a whole 2x2x4 slice. The times are simulated.
32 devices in a mesh: scan: 2 (over y), ang: 4 (over z), row: 4 (over x, core).
Axes of the slice: x: 2, y: 2, z: 4, core: 2. Of those that a mesh axis runs over, the one named last changes fastest.
Arguments:
- projections: bfloat16 [8, 32, 2560], P(('scan', 'ang'), 'row'), parts along dimension 0, may hold values from 0 to 2
- flats: float32 [64, 2560], P(('scan', 'row')), parts along dimension 0, may hold values from 1 to 3
- block_start: int32 [4, 4], replicated, may hold values from 0 to 2528
- bp_weights: bfloat16 [4, 32, 1024], P(None, None, 'ang'), may hold values from -0.5 to 0.5
Outputs:
- recon: float32 [64, 1024], P(('scan', 'row'), 'ang'), parts along dimension 0
There are 2 independent parts, one for each index of `scan`. A program takes and returns all parts, laid end to end along the dimension named above; an argument that names none is the same for every part. Nothing has to cross between parts.
Inputs may be any that keep to these rules, and one draw needn't show every extreme that they name: block_start[a, r] is the first of the 32 detector columns that pixel region r reads at angle a.
All inputs are finite; a program needn't handle non-finite values.
Results may differ from a plain program's by a relative error of at most 0.009.
Values may be sent and summed in bfloat16 or wider, within the bound.
A program may use at most 64 MiB of HBM per device.

v0:
```python
import functools

import jax
import jax.numpy as jnp
import numpy as np
from jax import lax
from jax.experimental import pallas as pl
from jax.experimental.pallas import tpu as pltpu
from jax.sharding import PartitionSpec as P

HALO = 4
LANES = 128
FLAT_CUTS = 2
TABLE_CUTS = 2
CENTRE = 10
EARLY = 4
paganin_beta = 8.0
ramp_gain = 320.0


def filter_table(tile_rows, width, columns):
    u = np.arange(tile_rows, dtype=np.float64)
    v = np.arange(width, dtype=np.float64)
    lam = (4.0 * np.sin(np.pi * u / tile_rows) ** 2)[:, None] + (4.0 * np.sin(np.pi * v / width) ** 2)[None, :]
    folded = np.minimum(v, width - v)
    ramp = ramp_gain * (folded / width) * (0.5 + 0.5 * np.cos(2.0 * np.pi * folded / width))
    taps = np.real(np.fft.ifft2(ramp[None, :] / (1.0 + paganin_beta * lam)))
    lags = tile_rows // 2 + 1
    place = (np.arange(columns)[:, None] - np.arange(width)[None, :]) % width
    sign = np.where(np.arange(width) < width // LANES // 2 * LANES, 1.0, -1.0)
    return taps[:lags][:, place].reshape(lags * columns, width) * sign


def kernel(regions, tiles, starts, proj, flats, table, weights, out,
           starts_s, proj_v, flats_v, table_v, weights_v, xs, ys, sbuf, rbuf,
           load_sem, done_sem):
    rows, width = flats.shape
    blocks = width // LANES
    angles, cb, _ = weights.shape
    half = rows // 2
    cs = LANES // (2 * rows)
    shifts = cb // cs
    pairs = shifts // 2
    lags = rows + 1
    order = [(0, 0), (1, 0), *[(0, d) for d in range(1, rows)], (1, rows - 1), *[(1, d) for d in range(1, rows - 1)]]
    me = lax.axis_index("ang")
    row = lax.axis_index("row")

    def peer(step, delta):
        return {"ang": lax.rem(me + step, regions), "row": lax.rem(row + delta + tiles, tiles)}

    def when_there(delta, action):
        if delta == 0:
            action()
        else:
            pl.when(row > 0 if delta < 0 else row < tiles - 1)(action)

    start_load = pltpu.make_async_copy(starts, starts_s, load_sem.at[2])
    table_load = pltpu.make_async_copy(table, table_v, load_sem.at[3])
    weight_load = pltpu.make_async_copy(weights, weights_v, done_sem.at[0])

    def load_columns(begin, end, cuts, sem):
        for n in range(cuts):
            part = pl.ds((begin + n * (end - begin) // cuts) * LANES, (end - begin) // cuts * LANES)
            pltpu.make_async_copy(flats.at[:, part], flats_v.at[:, part], sem).start()
        part = pl.ds(begin * LANES, (end - begin) * LANES)
        pltpu.make_async_copy(proj.at[0, :, part], proj_v.at[:, part], sem).start()

    def columns_loaded(count, sem):
        both = xs.at[pl.ds(0, count * 3 // 2)]
        pltpu.make_async_copy(both, both, sem).wait()

    load_columns(0, CENTRE, 1, load_sem.at[0])
    load_columns(CENTRE, blocks, FLAT_CUTS, load_sem.at[1])
    start_load.start()
    for d in range(lags):
        for n in range(TABLE_CUTS):
            part = pl.ds(n * width // TABLE_CUTS, width // TABLE_CUTS)
            pltpu.make_async_copy(table.at[pl.ds(d * cs, cs), part], table_v.at[pl.ds(d * cs, cs), part], load_sem.at[3]).start()
    weight_load.start()

    barrier = pltpu.get_barrier_semaphore()
    def greet(delta):
        for step in range(regions):
            if (step, delta) != (0, 0):
                pl.semaphore_signal(barrier, inc=1, device_id=peer(step, delta), device_id_type=pl.DeviceIdType.MESH)

    for delta in (-1, 0, 1):
        when_there(delta, lambda: greet(delta))

    def slot(delta):
        return pl.ds((1 + delta) * rows, rows)

    zeros = jnp.zeros((angles, rows, pairs * LANES), jnp.bfloat16)
    pl.when(row == tiles - 1)(lambda: rbuf.at[:, slot(-1)].__setitem__(..., zeros))
    pl.when(row == 0)(lambda: rbuf.at[:, slot(1)].__setitem__(..., zeros))

    lane = lax.broadcasted_iota(jnp.int32, (rows, LANES), 1)
    sub = lax.broadcasted_iota(jnp.int32, (rows, LANES), 0)

    pieces = [slice(b * LANES, (b + 1) * LANES) for b in range(blocks)]

    def contrast_of(p):
        return 1.0 - proj_v[:, p].astype(jnp.float32) / flats_v[:, p]

    columns_loaded(CENTRE, load_sem.at[0])
    contrast = [contrast_of(p) for p in pieces[:CENTRE]]
    centre = jnp.sum(sum(contrast), axis=1, keepdims=True) / (CENTRE * LANES)
    columns_loaded(blocks - CENTRE, load_sem.at[1])
    start_load.wait()

    contrast += [contrast_of(p) for p in pieces[CENTRE:]]
    for b, x in enumerate(contrast):
        xs[b] = x - centre
        xs[b + blocks] = x - centre

    spot = lane // cs
    lag = jnp.where(spot < 2, 0, jnp.where(spot < rows, spot - 1, jnp.where(spot < rows + 2, rows - 1, spot - rows - 1)))
    odd = (spot == 1) | (spot > rows)
    up, down = lax.rem(sub + rows - lag, rows), lax.rem(sub + lag, rows)
    inside = [sub >= lag, (lag > 0) & (sub + lag < rows)]
    wrapped = [(sub < lag) | (lag == 0), sub + lag >= rows]
    parts = {-1: [wrapped[0] & (up < half), wrapped[1] & (down < half)],
             1: [wrapped[0] & (up >= half), wrapped[1] & (down >= half)],
             0: inside}
    bits = [1 << n for n in range((rows - 1).bit_length())]
    deep = shifts * rows

    def shifted_rows(group, members=range(blocks)):
        used = sorted({b + n for b in members for n in (0, 1)})
        for region in group:
            shifted = []
            for k in range(shifts):
                start = starts_s[me, region] + k * cs
                first = start // LANES
                rest = lax.rem(start, LANES)
                shift = lax.rem(LANES - rest, LANES)
                low = lane < LANES - rest
                turned = {b: pltpu.roll(xs[first + b], shift, 1) for b in used}
                shifted.append({b: jnp.where(low, turned[b], turned[b + 1]) for b in members})
            for b in members:
                place = region * deep
                ys[place:place + deep, pieces[b]] = jnp.concatenate(
                    [y[b] for y in shifted], axis=0).astype(jnp.bfloat16)

    def filtered(group):
        cut = blocks // 2 * LANES
        begin = group[0] * deep
        end = begin + len(group) * deep
        near, far = (lax.dot_general(
            ys[begin:end, part], jnp.concatenate([table_v[d * cs:(d + 1) * cs, part] for _, d in [*order, (0, rows), (1, rows)]], axis=0),
            (((1,), (1,)), ((), ())), preferred_element_type=jnp.float32) for part in (slice(cut), slice(cut, width)))
        total = near - far
        total = jnp.concatenate([total, jnp.zeros((total.shape[0], LANES - 2 * cs), jnp.float32)], axis=1)
        for n, region in enumerate(group):
            for k in range(pairs):
                base = n * deep + k * 2 * rows
                even_rows, odd_rows = total[base:base + rows], total[base + rows:base + 2 * rows]
                tile = jnp.where(odd, odd_rows[:, :LANES], even_rows[:, :LANES])
                last = jnp.where(odd, odd_rows[:, LANES:], even_rows[:, LANES:])
                ahead, back = tile, tile
                for bit in bits:
                    turn = (lag & bit) > 0
                    ahead = jnp.where(turn, pltpu.roll(ahead, bit, 0), ahead)
                    back = jnp.where(turn, pltpu.roll(back, rows - bit, 0), back)
                edge = jnp.where(lag == 0, last, ahead)
                for delta, (first, second) in parts.items():
                    value = jnp.where(first, edge if delta else ahead, 0.0) + jnp.where(second, back, 0.0)
                    sbuf[(1 + delta) * regions + region, :, k * LANES:(k + 1) * LANES] = value.astype(jnp.bfloat16)

    def send(group):
        for region in group:
            last = (region + (regions - 1 if region < regions // 2 else 1)) % regions
            final = (me == last).astype(jnp.int32)
            for delta in (-1, 1, 0):
                copy = pltpu.make_async_remote_copy(
                    src_ref=sbuf.at[(1 + delta) * regions + region], dst_ref=rbuf.at[me, slot(delta)],
                    send_sem=done_sem.at[0], recv_sem=done_sem.at[final],
                    device_id={"ang": region, "row": lax.rem(row + delta + tiles, tiles)},
                    device_id_type=pl.DeviceIdType.MESH)
                if delta == 0:
                    pl.when(me != region)(copy.start)
                else:
                    when_there(delta, copy.start)

    early = [b for b in range(blocks) if b % (blocks // 2) < EARLY]
    shifted_rows([0], early)
    table_load.wait()
    shifted_rows([0], [b for b in range(blocks) if b not in early])
    filtered([0])
    sides = (row > 0).astype(jnp.int32) + (row < tiles - 1).astype(jnp.int32)
    pl.semaphore_wait(barrier, regions - 1 + sides * regions)
    send([0])
    shifted_rows([*range(1, regions)])
    filtered([*range(1, regions)])
    send([*range(1, regions)])
    rbuf[me, slot(0)] = sbuf[regions + me]

    inner = (row > 0) & (row < tiles - 1)
    turn = jnp.where(me < regions // 2, 1, regions - 1)

    def source(step):
        return lax.rem(me + step * turn, regions)

    def settled(full, short, sem):
        def wait(count):
            units = sbuf.at[pl.ds(0, count)]
            pltpu.make_async_copy(units, units, done_sem.at[sem]).wait()

        pl.when(inner)(lambda: wait(full))
        pl.when(jnp.logical_not(inner))(lambda: wait(short))

    def projected(steps):
        sums = []
        for half_pixels in range(2):
            pixels = pl.ds(half_pixels * (out.shape[1] // 2), out.shape[1] // 2)
            result = 0.0
            for step in steps:
                angle = source(step)
                w = jnp.concatenate(
                    [weights_v[angle, (2 * k + side) * cs:(2 * k + side + 1) * cs, pixels]
                     for k in range(pairs) for side, _ in order], axis=0)
                result += jnp.dot(rbuf[angle], w, preferred_element_type=jnp.float32)
            sums.append(result[:rows] + result[rows:2 * rows] + result[2 * rows:])
        return jnp.concatenate(sums, axis=1)

    loaded = angles * cb * out.shape[1] // (rows * pairs * LANES)
    settled(loaded + 6 * regions - 5, loaded + 4 * regions - 4, 0)
    out[...] = projected(range(regions - 1))
    settled(3, 2, 1)
    out[...] += projected([regions - 1])


def body(projections, flats, block_start, bp_weights):
    _, rows, width = projections.shape
    angles, cb, pixels = bp_weights.shape
    regions, tiles = lax.axis_size("ang"), lax.axis_size("row")
    cs = LANES // (2 * rows)
    pairs = cb // cs // 2
    table = jnp.asarray(filter_table(rows + 2 * HALO, width, cs), jnp.bfloat16)
    hbm = pl.BlockSpec(memory_space=pltpu.HBM)
    return pl.pallas_call(
        functools.partial(kernel, regions, tiles),
        name="fbp",
        out_shape=pltpu.VMEM((rows, pixels), jnp.float32),
        in_specs=[hbm, hbm, hbm, hbm, hbm],
        out_specs=pl.BlockSpec(memory_space=pltpu.VMEM),
        scratch_shapes=[
            pltpu.SMEM(block_start.shape, jnp.int32),
            pltpu.VMEM((rows, width), jnp.bfloat16),
            pltpu.VMEM((rows, width), jnp.float32),
            pltpu.VMEM(table.shape, jnp.bfloat16),
            pltpu.VMEM(bp_weights.shape, jnp.bfloat16),
            pltpu.VMEM((2 * width // LANES, rows, LANES), jnp.float32),
            pltpu.VMEM((regions * (cb // cs) * rows, width), jnp.bfloat16),
            pltpu.VMEM((6 * regions + bp_weights.size // (rows * pairs * LANES), rows, pairs * LANES), jnp.bfloat16),
            pltpu.VMEM((angles, 3 * rows, pairs * LANES), jnp.bfloat16),
            pltpu.SemaphoreType.DMA((4,)),
            pltpu.SemaphoreType.DMA((2,)),
        ],
        compiler_params=pltpu.CompilerParams(collective_id=0, has_side_effects=True, vmem_limit_bytes=65000000),
    )(block_start, projections, flats, table, bp_weights)


def solution(mesh):
    placed = (P(("scan", "ang"), "row", None), P(("scan", "row"), None), P(), P(None, None, "ang"))
    return jax.shard_map(
        body, mesh=mesh, in_specs=placed, out_specs=P(("scan", "row"), "ang"), check_vma=False
    )
```

profile of v0, /device:TPU:1, one launch (start us, length us, event | category | flops | bytes accessed | tf_op | source)
XLA Modules:
  0.0 9.1 jit_solution(10627586637254145973)
XLA Ops:
  0.0 8.5 %fbp.1 = f32[8,256]{1,0:T(8,128)S(1)} custom-call(s32[4,4]{1,0:T(4,128)} %starts.1, bf16[1,8,2560]{2,1,0:T(8,128)(2,1)} %proj.1, f32[8,2560]{1,0:T(8,128)} %flats.1, bf16[72,2560]{1,0:T(8,128)(2,1)} %constant.2.clone.table, bf16[4,32,256]{2,1,0:T(8,128)(2,1)} %weights.1), custom_call_target="tpu_custom_call" | custom-call | tf_op jit(solution)/shard_map/fbp/pallas_call | solution.py:242
  8.5 0.6 %copy.7 = f32[8,256]{1,0:T(8,128)} copy(f32[8,256]{1,0:T(8,128)S(1)} %fbp.1) | data formatting | bytes 16384
where the time goes:
time: 9.24 us; the launch traced here: 9.08 us
  Pallas kernels  8.47 us (92%)
  local copies, waits for them, and re-layouts  0.6 us (6%)
    pallas_call x1, Pallas kernels, body(): pl.pallas_call(functools.partial(kernel, regions, tiles), name='fbp', out...  8.47 us
    unnamed x1, local copies, waits for them, and re-layouts  0.6 us

commit v1 on v0

--- a/solution.py
+++ b/solution.py
@@ -13,7 +13,7 @@
 FLAT_CUTS = 2
 TABLE_CUTS = 2
 CENTRE = 10
-EARLY = 4
+EARLY = 6
 paganin_beta = 8.0
 ramp_gain = 320.0
 

time: 9.24 us -> 9.24 us (level)
  no operation moved by 1% of the time
where the time goes in v1:
time: 9.24 us; the launch traced here: 9.09 us
  Pallas kernels  8.48 us (92%)
  local copies, waits for them, and re-layouts  0.6 us (6%)
    pallas_call x1, Pallas kernels, body(): pl.pallas_call(functools.partial(kernel, regions, tiles), name='fbp', out...  8.48 us
    unnamed x1, local copies, waits for them, and re-layouts  0.6 us

profile of v1, /device:TPU:1, one launch (start us, length us, event | category | flops | bytes accessed | tf_op | source)
XLA Modules:
  0.0 9.1 jit_solution(2257037544028304253)
XLA Ops:
  0.0 8.5 %fbp.1 = f32[8,256]{1,0:T(8,128)S(1)} custom-call(s32[4,4]{1,0:T(4,128)} %starts.1, bf16[1,8,2560]{2,1,0:T(8,128)(2,1)} %proj.1, f32[8,2560]{1,0:T(8,128)} %flats.1, bf16[72,2560]{1,0:T(8,128)(2,1)} %constant.2.clone.table, bf16[4,32,256]{2,1,0:T(8,128)(2,1)} %weights.1), custom_call_target="tpu_custom_call" | custom-call | tf_op jit(solution)/shard_map/fbp/pallas_call | solution.py:242
  8.5 0.6 %copy.7 = f32[8,256]{1,0:T(8,128)} copy(f32[8,256]{1,0:T(8,128)S(1)} %fbp.1) | data formatting | bytes 16384

commit v2 on v0

--- a/solution.py
+++ b/solution.py
@@ -10,7 +10,7 @@
 
 HALO = 4
 LANES = 128
-FLAT_CUTS = 2
+FLAT_CUTS = 1
 TABLE_CUTS = 2
 CENTRE = 10
 EARLY = 4

time: 9.24 us -> 9.24 us (level)
  no operation moved by 1% of the time
where the time goes in v2:
time: 9.24 us; the launch traced here: 9.08 us
  Pallas kernels  8.47 us (92%)
  local copies, waits for them, and re-layouts  0.6 us (6%)
    pallas_call x1, Pallas kernels, body(): pl.pallas_call(functools.partial(kernel, regions, tiles), name='fbp', out...  8.47 us
    unnamed x1, local copies, waits for them, and re-layouts  0.6 us

profile of v2, /device:TPU:1, one launch (start us, length us, event | category | flops | bytes accessed | tf_op | source)
XLA Modules:
  0.0 9.1 jit_solution(14917059213427291198)
XLA Ops:
  0.0 8.5 %fbp.1 = f32[8,256]{1,0:T(8,128)S(1)} custom-call(s32[4,4]{1,0:T(4,128)} %starts.1, bf16[1,8,2560]{2,1,0:T(8,128)(2,1)} %proj.1, f32[8,2560]{1,0:T(8,128)} %flats.1, bf16[72,2560]{1,0:T(8,128)(2,1)} %constant.2.clone.table, bf16[4,32,256]{2,1,0:T(8,128)(2,1)} %weights.1), custom_call_target="tpu_custom_call" | custom-call | tf_op jit(solution)/shard_map/fbp/pallas_call | solution.py:242
  8.5 0.6 %copy.7 = f32[8,256]{1,0:T(8,128)} copy(f32[8,256]{1,0:T(8,128)S(1)} %fbp.1) | data formatting | bytes 16384

commit v3 on v0

--- a/solution.py
+++ b/solution.py
@@ -11,7 +11,7 @@
 HALO = 4
 LANES = 128
 FLAT_CUTS = 2
-TABLE_CUTS = 2
+TABLE_CUTS = 4
 CENTRE = 10
 EARLY = 4
 paganin_beta = 8.0

time: 9.24 us -> 9.24 us (level)
  no operation moved by 1% of the time
where the time goes in v3:
time: 9.24 us; the launch traced here: 9.08 us
  Pallas kernels  8.47 us (92%)
  local copies, waits for them, and re-layouts  0.6 us (6%)
    pallas_call x1, Pallas kernels, body(): pl.pallas_call(functools.partial(kernel, regions, tiles), name='fbp', out...  8.47 us
    unnamed x1, local copies, waits for them, and re-layouts  0.6 us

profile of v3, /device:TPU:1, one launch (start us, length us, event | category | flops | bytes accessed | tf_op | source)
XLA Modules:
  0.0 9.1 jit_solution(7794251548682180559)
XLA Ops:
  0.0 8.5 %fbp.1 = f32[8,256]{1,0:T(8,128)S(1)} custom-call(s32[4,4]{1,0:T(4,128)} %starts.1, bf16[1,8,2560]{2,1,0:T(8,128)(2,1)} %proj.1, f32[8,2560]{1,0:T(8,128)} %flats.1, bf16[72,2560]{1,0:T(8,128)(2,1)} %constant.2.clone.table, bf16[4,32,256]{2,1,0:T(8,128)(2,1)} %weights.1), custom_call_target="tpu_custom_call" | custom-call | tf_op jit(solution)/shard_map/fbp/pallas_call | solution.py:242
  8.5 0.6 %copy.7 = f32[8,256]{1,0:T(8,128)} copy(f32[8,256]{1,0:T(8,128)S(1)} %fbp.1) | data formatting | bytes 16384

commit v4 on v1

--- a/solution.py
+++ b/solution.py
@@ -12,7 +12,7 @@
 LANES = 128
 FLAT_CUTS = 2
 TABLE_CUTS = 2
-CENTRE = 10
+CENTRE = 8
 EARLY = 6
 paganin_beta = 8.0
 ramp_gain = 320.0

time: 9.24 us -> 9.22 us (level)
  no operation moved by 1% of the time
where the time goes in v4:
time: 9.22 us; the launch traced here: 9.06 us
  Pallas kernels  8.45 us (92%)
  local copies, waits for them, and re-layouts  0.6 us (7%)
    pallas_call x1, Pallas kernels, body(): pl.pallas_call(functools.partial(kernel, regions, tiles), name='fbp', out...  8.45 us
    unnamed x1, local copies, waits for them, and re-layouts  0.6 us

profile of v4, /device:TPU:1, one launch (start us, length us, event | category | flops | bytes accessed | tf_op | source)
XLA Modules:
  0.0 9.1 jit_solution(9432580300931271665)
XLA Ops:
  0.0 8.5 %fbp.1 = f32[8,256]{1,0:T(8,128)S(1)} custom-call(s32[4,4]{1,0:T(4,128)} %starts.1, bf16[1,8,2560]{2,1,0:T(8,128)(2,1)} %proj.1, f32[8,2560]{1,0:T(8,128)} %flats.1, bf16[72,2560]{1,0:T(8,128)(2,1)} %constant.2.clone.table, bf16[4,32,256]{2,1,0:T(8,128)(2,1)} %weights.1), custom_call_target="tpu_custom_call" | custom-call | tf_op jit(solution)/shard_map/fbp/pallas_call | solution.py:242
  8.5 0.6 %copy.7 = f32[8,256]{1,0:T(8,128)} copy(f32[8,256]{1,0:T(8,128)S(1)} %fbp.1) | data formatting | bytes 16384

commit v5 on v4

--- a/solution.py
+++ b/solution.py
@@ -13,7 +13,7 @@
 FLAT_CUTS = 2
 TABLE_CUTS = 2
 CENTRE = 8
-EARLY = 6
+EARLY = 4
 paganin_beta = 8.0
 ramp_gain = 320.0
 

time: 9.22 us -> 9.22 us (level)
  no operation moved by 1% of the time
where the time goes in v5:
time: 9.22 us; the launch traced here: 9.06 us
  Pallas kernels  8.45 us (92%)
  local copies, waits for them, and re-layouts  0.6 us (7%)
    pallas_call x1, Pallas kernels, body(): pl.pallas_call(functools.partial(kernel, regions, tiles), name='fbp', out...  8.45 us
    unnamed x1, local copies, waits for them, and re-layouts  0.6 us

profile of v5, /device:TPU:1, one launch (start us, length us, event | category | flops | bytes accessed | tf_op | source)
XLA Modules:
  0.0 9.1 jit_solution(7282264832470969736)
XLA Ops:
  0.0 8.5 %fbp.1 = f32[8,256]{1,0:T(8,128)S(1)} custom-call(s32[4,4]{1,0:T(4,128)} %starts.1, bf16[1,8,2560]{2,1,0:T(8,128)(2,1)} %proj.1, f32[8,2560]{1,0:T(8,128)} %flats.1, bf16[72,2560]{1,0:T(8,128)(2,1)} %constant.2.clone.table, bf16[4,32,256]{2,1,0:T(8,128)(2,1)} %weights.1), custom_call_target="tpu_custom_call" | custom-call | tf_op jit(solution)/shard_map/fbp/pallas_call | solution.py:242
  8.5 0.6 %copy.7 = f32[8,256]{1,0:T(8,128)} copy(f32[8,256]{1,0:T(8,128)S(1)} %fbp.1) | data formatting | bytes 16384
